TPU v7x, 32 devices: a whole 2x2x4 slice. The times are simulated.
32 devices in a mesh: scale: 2 (over y), lat: 16 (over z, x, core).
Axes of the slice: x: 2, y: 2, z: 4, core: 2. Of those that a mesh axis runs over, the one named last changes fastest.
Arguments:
- fine_state: float32 [16, 2, 1280, 1280], P(None, None, ('scale', 'lat')), may hold values from -6 to 6
- fine_noise: bfloat16 [16, 2, 1280, 1280], P(None, None, ('scale', 'lat')), may hold values from -6 to 6
- medium_state: float32 [16, 2, 640, 640], P(None, None, ('scale', 'lat')), may hold values from -6 to 6
- medium_noise: bfloat16 [16, 2, 640, 640], P(None, None, ('scale', 'lat')), may hold values from -6 to 6
- coarse_state: float32 [16, 2, 160, 160], P('lat'), may hold values from -6 to 6
- coarse_noise: bfloat16 [16, 2, 160, 160], P('lat'), may hold values from -6 to 6
- decay: float32 [3], replicated, may hold values from 0.5 to 0.95
- amplitude: float32 [3], replicated, may hold values from 0.3 to 1
- fine_basis: bfloat16 [1280, 32, 1280], P(('scale', 'lat')), may hold values from -0.0017089844 to 0.0017089844
- medium_basis: bfloat16 [640, 32, 640], P(('scale', 'lat')), may hold values from -0.0034179688 to 0.0034179688
- coarse_basis: bfloat16 [32, 160, 160], P(('scale', 'lat')), may hold values from -0.013671875 to 0.013671875
Outputs:
- fine_next: float32 [16, 2, 1280, 1280], P(None, None, ('scale', 'lat'))
- medium_next: float32 [16, 2, 640, 640], P(None, None, ('scale', 'lat'))
- coarse_next: float32 [16, 2, 160, 160], P('lat')
- pattern: float32 [16, 32, 2560], P(None, ('scale', 'lat'))
All inputs are finite; a program needn't handle non-finite values.
Results may differ from a plain program's by a relative error of at most 0.005.
Values may be sent and summed in bfloat16 or wider, within the bound.
A program may use at most 128 MiB of HBM per device.

v0:
```python
import math

import jax
import jax.numpy as jnp
from jax import lax
from jax.sharding import PartitionSpec as P

NLON = 2560


def advance(state, noise, decay_rate, amp_rate, offset):
    slots = state.shape[3]
    mode_ids = offset + jnp.arange(state.shape[2], dtype=jnp.int32)
    degree_ids = jnp.arange(slots, dtype=jnp.int32)
    inside = mode_ids[:, None] + degree_ids[None, :] < slots
    updated = decay_rate * state + amp_rate * noise.astype(jnp.float32)
    return jnp.where(inside, updated, jnp.zeros_like(updated))


def grid_table(mode_ids):
    lon_ids = jnp.arange(NLON, dtype=jnp.int32)
    angles = (mode_ids[:, None] * lon_ids[None, :] % NLON).astype(jnp.float32) * (
        2.0 * math.pi / NLON
    )
    weights = jnp.where(mode_ids == 0, 1.0, 2.0).astype(jnp.float32)[:, None]
    return jnp.stack([weights * jnp.cos(angles), -weights * jnp.sin(angles)]).astype(jnp.bfloat16)


def synthesis(fourier):
    table = grid_table(jnp.arange(fourier.shape[2], dtype=jnp.int32))
    return jnp.einsum("ecmr,cml->erl", fourier, table, preferred_element_type=jnp.float32)


def body(
    fine_state,
    fine_noise,
    medium_state,
    medium_noise,
    coarse_state,
    coarse_noise,
    decay,
    amplitude,
    fine_basis,
    medium_basis,
    coarse_basis,
):
    place = lax.axis_index(("scale", "lat"))
    fine_next = advance(fine_state, fine_noise, decay[0], amplitude[0], place * fine_state.shape[2])
    medium_next = advance(
        medium_state, medium_noise, decay[1], amplitude[1], place * medium_state.shape[2]
    )
    coarse_next = advance(coarse_state, coarse_noise, decay[2], amplitude[2], 0)
    fine_fourier = jnp.einsum(
        "ecmk,mrk->ecmr",
        fine_next.astype(jnp.bfloat16),
        fine_basis,
        preferred_element_type=jnp.float32,
    ).astype(jnp.bfloat16)
    medium_fourier = jnp.einsum(
        "ecmk,mrk->ecmr",
        medium_next.astype(jnp.bfloat16),
        medium_basis,
        preferred_element_type=jnp.float32,
    ).astype(jnp.bfloat16)
    coarse_half = coarse_next.astype(jnp.bfloat16)
    coarse_fourier = jnp.einsum(
        "ecmk,rmk->ecmr",
        lax.all_gather(coarse_half, "lat", axis=0, tiled=True),
        coarse_basis,
        preferred_element_type=jnp.float32,
    ).astype(jnp.bfloat16)
    fine_grid = synthesis(
        lax.all_to_all(fine_fourier, ("scale", "lat"), split_axis=3, concat_axis=2, tiled=True)
    )
    medium_grid = synthesis(
        lax.all_to_all(medium_fourier, ("scale", "lat"), split_axis=3, concat_axis=2, tiled=True)
    )
    total = fine_grid + medium_grid + synthesis(coarse_fourier)
    pattern = jnp.tanh(total)
    return (fine_next, medium_next, coarse_next, pattern)


def solution(mesh):
    return jax.shard_map(
        body,
        mesh=mesh,
        in_specs=(
            P(None, None, ("scale", "lat"), None),
            P(None, None, ("scale", "lat"), None),
            P(None, None, ("scale", "lat"), None),
            P(None, None, ("scale", "lat"), None),
            P("lat", None, None, None),
            P("lat", None, None, None),
            P(),
            P(),
            P(("scale", "lat"), None, None),
            P(("scale", "lat"), None, None),
            P(("scale", "lat"), None, None),
        ),
        out_specs=(
            P(None, None, ("scale", "lat"), None),
            P(None, None, ("scale", "lat"), None),
            P("lat", None, None, None),
            P(None, ("scale", "lat"), None),
        ),
        check_vma=False,
    )
```

profile of v0, /device:TPU:0, one launch (start us, length us, event | category | flops | bytes accessed | tf_op | source)
XLA Modules:
  0.0 170.2 jit_solution(12608711568485945702)
XLA Ops:
  7.2 0.1 add_compare_fusion.2
  7.3 1.5 fusion.70
  8.8 1.4 fusion.71
  10.1 5.5 %fusion.69 = (bf16[16,2,20,640]{3,1,2,0:T(2,128)(2,1)S(1)}, f32[16,2,20,640]{3,1,2,0:T(2,128)}) fusion(bf16[16,2,20,640]{3,1,2,0:T(2,128)(2,1)} %param.14, f32[]{:T(128)} %bitcast.3, f32[16,2,20,640]{3,1,2,0:T(2,128)} %param.13, f32[]{:T(128)} %bitcast.2, pred[20,640]{1,0:T(8,128)(4,1)S(1)} %add_compare_fusion.2), kind=kLoop, calls=%fused_computation.80 | loop fusion | flops 2457600 | bytes 4928008 | tf_op jit(solution)/shard_map/convert_element_type | solution.py:61
  15.6 1.1 fusion.53
  16.7 1.5 copy.34
  18.1 0.9 reshape.367
  19.1 7.4 %all-to-all-start.1 = ((bf16[32,2,320]{2,1,0:T(2,128)(2,1)}), bf16[32,2,320]{2,1,0:T(2,128)(2,1)}, u32[]{:S(2)}, u32[]{:S(2)}) async-start(bf16[32,2,320]{2,1,0:T(2,128)(2,1)} %reshape.367), calls=%async_computation.1 | async-start | bytes 98304 | tf_op jit(solution)/shard_map/all_to_all | solution.py:76
  26.5 0.0 all-gather.2.cloned.1.call-start
  26.6 3.1 %fusion.67 = (bf16[1,2,160,160]{3,2,1,0:T(8,128)(2,1)}, f32[1,2,160,160]{3,2,1,0:T(8,128)}) fusion(bf16[1,2,160,160]{3,2,1,0:T(8,128)(2,1)} %param.16, f32[]{:T(128)} %bitcast.5, f32[1,2,160,160]{3,2,1,0:T(8,128)} %param.15, f32[]{:T(128)} %bitcast.4, pred[160,160]{1,0:T(8,128)(4,1)S(1)} %add_compare_fusion.1), kind=kLoop, calls=%fused_computation.78 | loop fusion | flops 307200 | bytes 640008 | tf_op jit(solution)/shard_map/convert_element_type | solution.py:65
  29.8 0.1 add_compare_fusion
  30.0 28.5 %multiply_convert_fusion.2 = (bf16[1,640,2560]{2,1,0:T(8,128)(2,1)}, bf16[1,640,2560]{2,1,0:T(8,128)(2,1)}) fusion(f32[640]{0:T(1024)S(1)} %fusion.62, f32[640]{0:T(1024)S(1)} %fusion.60), kind=kLoop, calls=%fused_computation.20 | loop fusion | flops 21299200 | bytes 6558720 | tf_op jit(solution)/shard_map/convert.3
  58.5 56.2 %multiply_convert_fusion = (bf16[1,1280,2560]{2,1,0:T(8,128)(2,1)}, bf16[1,1280,2560]{2,1,0:T(8,128)(2,1)}) fusion(f32[1280]{0:T(1024)S(1)} %fusion.61, f32[1280]{0:T(1024)S(1)} %fusion.59), kind=kLoop, calls=%fused_computation.7 | loop fusion | flops 42598400 | bytes 13117440 | tf_op jit(solution)/shard_map/convert.5
  114.7 7.7 %multiply_convert_fusion.4 = (bf16[1,160,2560]{2,1,0:T(8,128)(2,1)}, bf16[1,160,2560]{2,1,0:T(8,128)(2,1)}) fusion(f32[160]{0:T(256)S(1)} %fusion.63, f32[160]{0:T(256)S(1)} %compare_select_fusion), kind=kLoop, calls=%fused_computation.45 | loop fusion | flops 5324800 | bytes 1639680 | tf_op jit(solution)/shard_map/convert.1
  122.4 5.5 %fusion.68 = (bf16[16,2,40,1280]{3,2,1,0:T(8,128)(2,1)S(1)}, f32[16,2,40,1280]{3,2,1,0:T(8,128)}) fusion(bf16[16,2,40,1280]{3,2,1,0:T(8,128)(2,1)S(1)} %copy-done.1, f32[]{:T(128)} %bitcast.1, f32[16,2,40,1280]{3,2,1,0:T(8,128)S(1)} %bitcast.80, f32[]{:T(128)} %bitcast, pred[40,1280]{1,0:T(8,128)(4,1)S(1)} %add_compare_fusion), kind=kLoop, calls=%fused_computation.79 | loop fusion | flops 9830400 | bytes 19712008 | tf_op jit(solution)/shard_map/convert_element_type | solution.py:55
  127.9 2.0 %fusion.48 = bf16[16,2,40,32]{3,0,1,2:T(8,128)(2,1)} fusion(bf16[40,32,1280]{2,1,0:T(8,128)(2,1)S(1)} %copy-done, bf16[16,2,40,1280]{3,2,1,0:T(8,128)(2,1)S(1)} %get-tuple-element.22), kind=kOutput, calls=%fused_computation.53 | convolution fusion | flops 104898560 | bytes 6635520 | tf_op jit(solution)/shard_map/ecmk,mrk->ecmr/dot_general | solution.py:53
  130.0 1.6 copy.31
  131.5 1.0 reshape.369
  132.5 6.1 %all-to-all-start = ((bf16[32,2,640]{2,1,0:T(2,128)(2,1)}), bf16[32,2,640]{2,1,0:T(2,128)(2,1)}, u32[]{:S(2)}, u32[]{:S(2)}) async-start(bf16[32,2,640]{2,1,0:T(2,128)(2,1)} %reshape.369), calls=%async_computation | async-start | bytes 163840 | tf_op jit(solution)/shard_map/all_to_all | solution.py:73
  138.6 1.2 reshape.368
  139.8 0.1 copy.35
  139.9 1.0 reshape.357
  140.9 4.6 %fusion.18 = f32[16,2560]{1,0:T(8,128)} fusion(bf16[16,2,640]{2,0,1:T(8,128)(2,1)} %reshape.357, bf16[1,640,2560]{2,1,0:T(8,128)(2,1)} %get-tuple-element.32, bf16[1,640,2560]{2,1,0:T(8,128)(2,1)} %get-tuple-element.33), kind=kOutput, calls=%fused_computation.27 | convolution fusion | flops 108134400 | bytes 6758400 | tf_op jit(solution)/shard_map/ecmr,cml->erl/dot_general | solution.py:31
  145.5 0.5 all-to-all-done
  146.0 1.3 reshape.370
  147.3 0.1 copy.32
  147.4 1.0 reshape.356
  148.4 7.4 %fusion.27 = f32[16,2560]{1,0:T(8,128)} fusion(f32[16,2560]{1,0:T(8,128)} %fusion.18, bf16[16,2,1280]{2,0,1:T(8,128)(2,1)} %reshape.356, bf16[1,1280,2560]{2,1,0:T(8,128)(2,1)} %get-tuple-element.34, bf16[1,1280,2560]{2,1,0:T(8,128)(2,1)} %get-tuple-element.35), kind=kOutput, calls=%fused_computation.33 | convolution fusion | flops 216309760 | bytes 13516800 | tf_op jit(solution)/shard_map/ecmr,cml->erl/dot_general | solution.py:31
  155.8 4.9 %fusion.33 = bf16[160,1,16,2]{2,1,3,0:T(2,128)(2,1)S(1)} fusion(bf16[16,2,160,160]{3,2,1,0:T(8,128)(2,1)} %all-gather.2.cloned.1.call-done, bf16[160,160,1,1]{1,0,2,3:T(8,128)(2,1)S(1)} %bitcast.83), kind=kOutput, calls=%fused_computation.37 | convolution fusion | flops 1638400 | bytes 1699840 | tf_op jit(solution)/shard_map/ecmk,rmk->ecmr/dot_general | solution.py:66
  160.6 0.1 copy.41
  160.7 1.8 %fusion.26 = f32[16,1,2560]{2,0,1:T(8,128)S(1)} fusion(f32[16,2560]{1,0:T(8,128)} %fusion.27, bf16[1,160,2560]{2,1,0:T(8,128)(2,1)} %get-tuple-element.36, bf16[1,160,2560]{2,1,0:T(8,128)(2,1)} %get-tuple-element.37, bf16[160,1,16,2]{0,2,3,1:T(8,128)(2,1)S(1)} %copy.41), kind=kOutput, calls=%fused_computation.32 | convolution fusion | flops 27074560 | bytes 1976320 | tf_op jit(solution)/shard_map/ecmr,cml->erl/dot_general | solution.py:31
  162.6 0.8 copy.36
  (27 shorter events, 0.1 us)
Async XLA Ops:
  7.2 120.7 %copy-start = (bf16[40,32,1280]{2,1,0:T(8,128)(2,1)S(1)}, bf16[40,32,1280]{2,1,0:T(8,128)(2,1)}, u32[]{:S(2)}) copy-start(bf16[40,32,1280]{2,1,0:T(8,128)(2,1)} %param.19) | copy-start | bytes 9830404
  7.2 8.4 %copy-start.2 = (bf16[20,32,640]{2,1,0:T(8,128)(2,1)S(1)}, bf16[20,32,640]{2,1,0:T(8,128)(2,1)}, u32[]{:S(2)}) copy-start(bf16[20,32,640]{2,1,0:T(8,128)(2,1)} %param.20) | copy-start | bytes 2457604
  19.1 113.4 %all-to-all-start.1 = ((bf16[32,2,320]{2,1,0:T(2,128)(2,1)}), bf16[32,2,320]{2,1,0:T(2,128)(2,1)}, u32[]{:S(2)}, u32[]{:S(2)}) async-start(bf16[32,2,320]{2,1,0:T(2,128)(2,1)} %reshape.367), calls=%async_computation.1 | async-start | bytes 98304 | tf_op jit(solution)/shard_map/all_to_all | solution.py:76
  26.5 129.2 %all-gather.2.cloned.1.call-start = ((), (), s32[]{:S(2)}) async-start(), calls=%async_computation.2 | async-start | bytes 2785280 | tf_op jit(solution)/shard_map/all_gather | solution.py:68
  29.9 92.4 %slice-start = ((s8[6553600]{0:T(1024)(128)(4,1)}), s8[4194304]{0:T(1024)(128)(4,1)S(1)}, s32[]{:S(2)}) async-start(s8[6553600]{0:T(1024)(128)(4,1)} %bitcast.79), calls=%async_computation.3 | async-start | bytes 8388608
  58.5 63.9 %slice-start.1 = ((s8[6553600]{0:T(1024)(128)(4,1)}), s8[2359296]{0:T(1024)(128)(4,1)S(1)}, s32[]{:S(2)}) async-start(s8[6553600]{0:T(1024)(128)(4,1)} %bitcast.79), calls=%async_computation.4 | async-start | bytes 4718592
  58.5 63.9 %copy-start.1 = (bf16[16,2,40,1280]{3,2,1,0:T(8,128)(2,1)S(1)}, bf16[16,2,40,1280]{3,2,1,0:T(8,128)(2,1)}, u32[]{:S(2)}) copy-start(bf16[16,2,40,1280]{3,2,1,0:T(8,128)(2,1)} %param.12) | copy-start | bytes 9830404
  132.5 13.5 %all-to-all-start = ((bf16[32,2,640]{2,1,0:T(2,128)(2,1)}), bf16[32,2,640]{2,1,0:T(2,128)(2,1)}, u32[]{:S(2)}, u32[]{:S(2)}) async-start(bf16[32,2,640]{2,1,0:T(2,128)(2,1)} %reshape.369), calls=%async_computation | async-start | bytes 163840 | tf_op jit(solution)/shard_map/all_to_all | solution.py:73
  148.4 7.4 %copy-start.3 = (bf16[1,160,160]{2,1,0:T(8,128)(2,1)S(1)}, bf16[1,160,160]{2,1,0:T(8,128)(2,1)}, u32[]{:S(2)}) copy-start(bf16[1,160,160]{2,1,0:T(8,128)(2,1)} %param.21) | copy-start | bytes 153604
Sparse Core Ops, SparseCore 0:
  30.2 44.4 all-gather.1
where the time goes:
time: 171 us; the launch traced here: 170 us
  other arithmetic  107 us (63%)
  matrix products  21.8 us (13%)
  between operations  14.3 us (8%)
  starting transfers between devices  13.5 us (8%)
  local copies, waits for them, and re-layouts  13.4 us (8%)
    another operation x3, other arithmetic  92.4 us
    dot_general x3, matrix products, synthesis(): jnp.einsum('ecmr,cml->erl', fourier, table, preferred_element_type=jnp.fl...  13.8 us
    all_to_all x1, starting transfers between devices, body(): lax.all_to_all(medium_fourier, ('scale', 'lat'), split_axis=3, concat_axi...  7.44 us
    all_to_all x1, starting transfers between devices, body(): lax.all_to_all(fine_fourier, ('scale', 'lat'), split_axis=3, concat_axis=...  6.06 us
    convert_element_type x1, other arithmetic, body(): fine_next.astype(jnp.bfloat16)  5.5 us
    convert_element_type x1, other arithmetic, body(): medium_next.astype(jnp.bfloat16)  5.48 us
    unnamed x17, local copies, waits for them, and re-layouts  5.27 us
    dot_general x1, matrix products, body(): jnp.einsum('ecmk,rmk->ecmr', lax.all_gather(coarse_half, 'lat', axis=0, t...  4.89 us
  transfers between devices with their start and end apart: 3, of which 1 were waited for; matrix products, arithmetic and copies ran while one was open for 72% of the time, Pallas kernels for 0%

commit v1 on v0

v1 whole, which is shorter than its diff:
```python
import math

import jax
import jax.numpy as jnp
from jax import lax
from jax.sharding import PartitionSpec as P

NLON = 2560
LANES = 128
FOLD = NLON // LANES


def advance(state, noise, decay_rate, amp_rate, offset):
    slots = state.shape[3]
    mode_ids = offset + jnp.arange(state.shape[2], dtype=jnp.int32)
    degree_ids = jnp.arange(slots, dtype=jnp.int32)
    inside = mode_ids[:, None] + degree_ids[None, :] < slots
    updated = decay_rate * state + amp_rate * noise.astype(jnp.float32)
    return jnp.where(inside, updated, jnp.zeros_like(updated))


def angle_tables(high):
    lon = jnp.arange(LANES, dtype=jnp.int32)
    hi = (jnp.arange(high, dtype=jnp.int32)[:, None] * lon[None, :] % LANES).astype(jnp.float32)
    lo = (jnp.arange(FOLD, dtype=jnp.int32)[:, None] * lon[None, :]).astype(jnp.float32)
    hi, lo = lax.optimization_barrier(
        (
            jnp.stack([jnp.cos(hi * (2 * math.pi / LANES)), jnp.sin(hi * (2 * math.pi / LANES))]),
            jnp.stack([jnp.cos(lo * (2 * math.pi / NLON)), jnp.sin(lo * (2 * math.pi / NLON))]),
        )
    )
    ch, sh = hi[0][:, None, :], hi[1][:, None, :]
    cl, sl = lo[0][None], lo[1][None]
    first = (jnp.arange(high) == 0)[:, None, None] & (jnp.arange(FOLD) == 0)[None, :, None]
    weight = jnp.where(first, 1.0, 2.0).astype(jnp.float32)
    cos, sin = weight * (ch * cl - sh * sl), weight * (sh * cl + ch * sl)
    table = jnp.stack(
        [jnp.concatenate([cos, sin], axis=-1), jnp.concatenate([-sin, cos], axis=-1)]
    )
    return table.astype(jnp.bfloat16)


def body(
    fine_state,
    fine_noise,
    medium_state,
    medium_noise,
    coarse_state,
    coarse_noise,
    decay,
    amplitude,
    fine_basis,
    medium_basis,
    coarse_basis,
):
    place = lax.axis_index(("scale", "lat"))
    fine_next = advance(fine_state, fine_noise, decay[0], amplitude[0], place * fine_state.shape[2])
    medium_next = advance(
        medium_state, medium_noise, decay[1], amplitude[1], place * medium_state.shape[2]
    )
    coarse_next = advance(coarse_state, coarse_noise, decay[2], amplitude[2], 0)
    devices = lax.axis_size("scale") * lax.axis_size("lat")
    part_modes = -(-coarse_next.shape[2] // devices)
    modes = coarse_next.shape[2]
    grow = ((0, 0), (0, 0), (0, part_modes * devices - modes), (0, 0))
    held, own, slots = coarse_next.shape[0], coarse_basis.shape[0], coarse_next.shape[3]
    mine = jnp.concatenate(
        [coarse_next.astype(jnp.bfloat16).reshape(held * 2, modes, slots), coarse_basis], axis=0
    )
    mine = jnp.pad(mine, grow[1:]).reshape(-1, devices, part_modes * slots).swapaxes(0, 1)
    mixed = lax.all_to_all(mine, ("scale", "lat"), split_axis=0, concat_axis=0, tiled=True)
    mixed = mixed.reshape(devices, 2 * held + own, part_modes, slots)
    lat = lax.axis_size("lat")
    coarse_half = mixed[:lat, : 2 * held].reshape(lat * held, 2, part_modes, slots)
    coarse_rows = mixed[:, 2 * held :].reshape(devices * own, part_modes, slots)
    fourier = []
    for half, basis, form in (
        (fine_next.astype(jnp.bfloat16), fine_basis, "ecmk,mrk->rcme"),
        (medium_next.astype(jnp.bfloat16), medium_basis, "ecmk,mrk->rcme"),
        (coarse_half, coarse_rows, "ecmk,rmk->rcme"),
    ):
        fourier.append(
            jnp.einsum(form, half, basis, preferred_element_type=jnp.float32).astype(jnp.bfloat16)
        )
    members = coarse_half.shape[0]
    mf, mm = fine_state.shape[2], medium_state.shape[2]
    rows = fine_basis.shape[1]
    both = jnp.concatenate(fourier, axis=2).reshape(rows, 2, (mf + mm + part_modes) * members)
    got = lax.all_to_all(both, ("scale", "lat"), split_axis=0, concat_axis=0, tiled=True)
    got = got.reshape(devices, own, 2, mf + mm + part_modes, members)
    got = got.transpose(1, 2, 0, 3, 4)

    def fold(x):
        return x.reshape(own, 2, -1, FOLD, members)

    fine = fold(got[:, :, :, :mf])
    medium = fold(got[:, :, :, mf : mf + mm])
    coarse = got[:, :, :, mf + mm :].reshape(own, 2, devices * part_modes, members)
    coarse = fold(coarse[:, :, :modes])
    table = angle_tables(fine.shape[2])
    stacked = jnp.concatenate([fine, medium, coarse], axis=2)
    stacked_table = jnp.concatenate(
        [table, table[:, : medium.shape[2]], table[:, : coarse.shape[2]]], axis=1
    )
    part = jnp.einsum(
        "rchqe,chqx->reqx", stacked, stacked_table, preferred_element_type=jnp.float32
    ).reshape(own, members, FOLD, 2, LANES)
    angle = (
        (jnp.arange(FOLD)[:, None] * jnp.arange(FOLD)[None, :] % FOLD).astype(jnp.float32)
        * (2 * math.pi / FOLD)
    )
    turn = jnp.stack([jnp.cos(angle), -jnp.sin(angle)], axis=1)
    total = jnp.einsum("reqxl,qxh->erhl", part, turn, precision=lax.Precision.HIGHEST)
    pattern = jnp.tanh(total.reshape(members, own, NLON))
    return (fine_next, medium_next, coarse_next, pattern)


def solution(mesh):
    return jax.shard_map(
        body,
        mesh=mesh,
        in_specs=(
            P(None, None, ("scale", "lat"), None),
            P(None, None, ("scale", "lat"), None),
            P(None, None, ("scale", "lat"), None),
            P(None, None, ("scale", "lat"), None),
            P("lat", None, None, None),
            P("lat", None, None, None),
            P(),
            P(),
            P(("scale", "lat"), None, None),
            P(("scale", "lat"), None, None),
            P(("scale", "lat"), None, None),
        ),
        out_specs=(
            P(None, None, ("scale", "lat"), None),
            P(None, None, ("scale", "lat"), None),
            P("lat", None, None, None),
            P(None, ("scale", "lat"), None),
        ),
        check_vma=False,
    )
```

time: 171 us -> 78.2 us (0.46)
  other arithmetic: 107 us -> 23.9 us
  matrix products: 21.8 us -> 7.65 us
  between operations: 14.3 us -> 0.8 us
  local copies, waits for them, and re-layouts: 13.4 us -> 26.9 us
  waiting for transfers between devices: 0.52 us -> 4.94 us
    another operation x3 -> x5, other arithmetic: 92.4 us -> 3.74 us  [the longest x2 2.38 us: angle_tables(): jnp.stack([jnp.concatenate([cos, sin], axis=-1), jnp.concatenate([-sin, c...]
    dot_general x6 -> x5, matrix products: 21.8 us -> 7.65 us  [the longest x3 3.24 us: body(): jnp.einsum(form, half, basis, preferred_element_type=jnp.float32)]
    reshape x1 -> x5, local copies, waits for them, and re-layouts: 0.95 us -> 8.15 us  [the longest x2 3.13 us: fold(): return x.reshape(own, 2, -1, FOLD, members)]
    slice x0 -> x7, local copies, waits for them, and re-layouts: none -> 6.08 us  [the longest x2 2.07 us: body(): fine = fold(got[:, :, :, :mf])]
    all_to_all x2, waiting for transfers between devices: 0.5 us -> 4.94 us  [the longest x1 4.94 us: body(): lax.all_to_all(both, ('scale', 'lat'), split_axis=0, concat_axis=0, tiled...]
    unnamed x17 -> x18, local copies, waits for them, and re-layouts: 5.27 us -> 1.11 us
    convert_element_type x1, other arithmetic: 5.5 us -> 9.05 us  [body(): fine_next.astype(jnp.bfloat16)]
    convert_element_type x2 -> x0, local copies, waits for them, and re-layouts: 3.03 us -> none  [the longest x1 1.58 us: body(): fine_fourier = jnp.einsum('ecmk,mrk->ecmr', fine_next.astype(jnp.bfloat16...]
  transfers between devices with their start and end apart: 3 -> 2, of which waited for: 1 -> 1; matrix products, arithmetic and copies ran while one was open for 72% -> 31% of each run, Pallas kernels for 0% -> 0%
where the time goes in v1:
time: 78.2 us; the launch traced here: 77.4 us
  local copies, waits for them, and re-layouts  26.9 us (34%)
  other arithmetic  23.9 us (31%)
  starting transfers between devices  13.2 us (17%)
  matrix products  7.65 us (10%)
  waiting for transfers between devices  4.94 us (6%)
  between operations  0.8 us (1%)
    convert_element_type x1, other arithmetic, body(): fine_next.astype(jnp.bfloat16)  9.05 us
    all_to_all x1, starting transfers between devices, body(): lax.all_to_all(mine, ('scale', 'lat'), split_axis=0, concat_axis=0, tiled...  7.33 us
    all_to_all x1, starting transfers between devices, body(): lax.all_to_all(both, ('scale', 'lat'), split_axis=0, concat_axis=0, tiled...  5.83 us
    all_to_all x1, waiting for transfers between devices, body(): lax.all_to_all(both, ('scale', 'lat'), split_axis=0, concat_axis=0, tiled...  4.94 us
    convert_element_type x1, other arithmetic, body(): medium_next.astype(jnp.bfloat16)  3.77 us
    dot_general x3, matrix products, body(): jnp.einsum(form, half, basis, preferred_element_type=jnp.float32)  3.24 us
    convert_element_type x1, other arithmetic, body(): coarse_next.astype(jnp.bfloat16).reshape(held * 2, modes, slots)  3.15 us
    reshape x2, local copies, waits for them, and re-layouts, fold(): return x.reshape(own, 2, -1, FOLD, members)  3.13 us
  transfers between devices with their start and end apart: 2, of which 1 were waited for; matrix products, arithmetic and copies ran while one was open for 31% of the time, Pallas kernels for 0%

profile of v1, /device:TPU:0, one launch (start us, length us, event | category | flops | bytes accessed | tf_op | source)
XLA Modules:
  0.0 77.4 jit_solution(7409587576221621649)
XLA Ops:
  0.7 1.4 %fusion.56 = (f32[1]{0:T(128)}, f32[1]{0:T(128)}, f32[1]{0:T(128)}) fusion(f32[3]{0:T(128)} %param.17), kind=kLoop, calls=%fused_computation.86 | loop fusion | bytes 24 | tf_op jit(solution)/shard_map/slice | solution.py:61
  2.1 1.4 %fusion.57 = (f32[1]{0:T(128)}, f32[1]{0:T(128)}, f32[1]{0:T(128)}) fusion(f32[3]{0:T(128)} %param.18), kind=kLoop, calls=%fused_computation.87 | loop fusion | bytes 24 | tf_op jit(solution)/shard_map/slice | solution.py:61
  3.5 3.1 %fusion.55 = (bf16[1,2,160,160]{3,2,1,0:T(8,128)(2,1)S(1)}, f32[1,2,160,160]{3,2,1,0:T(8,128)}) fusion(bf16[1,2,160,160]{3,2,1,0:T(8,128)(2,1)} %param.16, f32[]{:T(128)} %bitcast.5, f32[1,2,160,160]{3,2,1,0:T(8,128)} %param.15, f32[]{:T(128)} %bitcast.4, pred[160,160]{1,0:T(8,128)(4,1)S(1)} %add_compare_fusion.1), kind=kLoop, calls=%fused_computation.85 | loop fusion | flops 307200 | bytes 640008 | tf_op jit(solution)/shard_map/convert_element_type | solution.py:68
  6.8 1.0 %concatenate.29 = bf16[1,32,800]{2,1,0:T(8,128)(2,1)S(1)} reshape(bf16[1,160,160]{2,1,0:T(8,128)(2,1)} %param.21) | data formatting | bytes 102400 | tf_op jit(solution)/shard_map/concatenate | solution.py:67
  7.9 0.8 %copy.75 = bf16[32,3,800]{2,1,0:T(4,128)(2,1)} copy(bf16[32,3,800]{2,0,1:T(8,128)(2,1)S(1)} %maximum_bitcast_fusion.2) | data formatting | bytes 307200 | tf_op jit(solution)/shard_map/transpose | solution.py:70
  8.7 7.3 %all-to-all-start = ((bf16[32,3,800]{2,1,0:T(4,128)(2,1)}), bf16[32,3,800]{2,1,0:T(4,128)(2,1)S(1)}, u32[]{:S(2)}, u32[]{:S(2)}) async-start(bf16[32,3,800]{2,1,0:T(4,128)(2,1)} %copy.75), calls=%async_computation | async-start | bytes 458752 | tf_op jit(solution)/shard_map/all_to_all | solution.py:71
  19.6 9.1 %fusion.53 = (bf16[16,2,40,1280]{3,2,1,0:T(8,128)(2,1)S(1)}, f32[16,2,40,1280]{3,2,1,0:T(8,128)}) fusion(bf16[16,2,40,1280]{3,2,1,0:T(8,128)(2,1)} %param.12, f32[]{:T(128)} %bitcast.1, f32[16,2,40,1280]{3,2,1,0:T(8,128)} %param.11, f32[]{:T(128)} %bitcast, pred[40,1280]{1,0:T(8,128)(4,1)} %add_compare_fusion), kind=kLoop, calls=%fused_computation.83 | loop fusion | flops 9830400 | bytes 19712008 | tf_op jit(solution)/shard_map/convert_element_type | solution.py:78
  28.6 2.0 %fusion.11 = bf16[32,2,40,16]{0,3,1,2:T(8,128)(2,1)} fusion(bf16[40,32,1280]{2,1,0:T(8,128)(2,1)S(1)} %copy-done, bf16[16,2,40,1280]{3,2,1,0:T(8,128)(2,1)S(1)} %get-tuple-element.28), kind=kOutput, calls=%fused_computation.11 | convolution fusion | flops 104898560 | bytes 6635520 | tf_op jit(solution)/shard_map/ecmk,mrk->rcme/dot_general | solution.py:83
  30.7 1.4 %fusion.26 = (bf16[64,20,128]{2,0,1:T(8,128)(2,1)}, bf16[64,20,128]{2,0,1:T(8,128)(2,1)}, bf16[64,20,128]{2,0,1:T(8,128)(2,1)}) fusion(f32[20,128]{1,0:T(8,128)S(1)} %copy-done.6, f32[64,128]{1,0:T(8,128)S(1)} %copy-done.5, f32[20,128]{1,0:T(8,128)S(1)} %get-tuple-element.41, f32[64,128]{1,0:T(8,128)S(1)} %get-tuple-element.39, f32[64,20]{0,1:T(8,128)S(1)} %and_select_fusion), kind=kLoop, calls=%fused_computation.27 | loop fusion | flops 1966080 | bytes 1074176 | tf_op jit(solution)/shard_map/convert.7
  32.1 3.8 %fusion.54 = (bf16[16,2,20,640]{3,1,2,0:T(2,128)(2,1)S(1)}, f32[16,2,20,640]{3,1,2,0:T(2,128)}) fusion(bf16[16,2,20,640]{3,1,2,0:T(2,128)(2,1)S(1)} %copy-done.4, f32[]{:T(128)} %bitcast.3, f32[16,2,20,640]{3,1,2,0:T(2,128)S(1)} %copy-done.3, f32[]{:T(128)} %bitcast.2, pred[20,640]{1,0:T(8,128)(4,1)S(1)} %add_compare_fusion.2), kind=kLoop, calls=%fused_computation.84 | loop fusion | flops 2457600 | bytes 4928008 | tf_op jit(solution)/shard_map/convert_element_type | solution.py:79
  36.5 1.1 %fusion.21 = bf16[32,2,20,16]{0,3,1,2:T(8,128)(2,1)} fusion(bf16[20,32,640]{2,1,0:T(8,128)(2,1)S(1)} %copy-done.8, bf16[16,2,20,640]{3,1,2,0:T(2,128)(2,1)S(1)} %get-tuple-element.30), kind=kOutput, calls=%fused_computation.17 | convolution fusion | flops 26234880 | bytes 1679360 | tf_op jit(solution)/shard_map/ecmk,mrk->rcme/dot_general | solution.py:83
  38.2 2.0 %reshape.262 = bf16[32,3,5,160]{3,2,0,1:T(8,128)(2,1)} reshape(bf16[32,3,800]{2,0,1:T(8,128)(2,1)} %copy.76) | data formatting | bytes 307200 | tf_op jit(solution)/shard_map/reshape | solution.py:72
  40.2 0.9 %slice.70 = bf16[32,1,5,160]{3,2,0,1:T(8,128)(2,1)S(1)} slice(bf16[32,3,5,160]{3,2,0,1:T(8,128)(2,1)} %reshape.262), slice={[0:32], [2:3], [0:5], [0:160]} | slice | bytes 102400 | tf_op jit(solution)/shard_map/slice | solution.py:75
  41.1 0.9 %slice.71 = bf16[16,2,5,160]{3,2,0,1:T(8,128)(2,1)S(1)} slice(bf16[32,3,5,160]{3,2,0,1:T(8,128)(2,1)} %reshape.262), slice={[0:16], [0:2], [0:5], [0:160]} | slice | bytes 102400 | tf_op jit(solution)/shard_map/slice | solution.py:74
  42.2 1.2 %pad_maximum_fusion.1 = bf16[32,2,65,16]{0,3,1,2:T(8,128)(2,1)S(1)} fusion(bf16[32,2,5,16]{0,3,1,2:T(8,128)(2,1)S(1)} %fusion.22, bf16[32,2,20,16]{0,3,1,2:T(8,128)(2,1)} %fusion.21, bf16[32,2,40,16]{0,3,1,2:T(8,128)(2,1)} %fusion.11), kind=kLoop, calls=%fused_computation.29 | loop fusion | flops 133120 | bytes 266240 | tf_op jit(solution)/shard_map/concatenate | solution.py:88
  43.4 0.9 %copy.79 = bf16[32,2,65,16]{0,3,2,1:T(8,128)(2,1)} copy(bf16[32,2,65,16]{0,3,1,2:T(8,128)(2,1)S(1)} %pad_maximum_fusion.1) | data formatting | bytes 266240 | tf_op jit(solution)/shard_map/concatenate | solution.py:88
  44.3 1.9 %copy.80 = bf16[32,2,1040]{2,1,0:T(2,128)(2,1)} copy(bf16[32,2,1040]{0,2,1:T(8,128)(2,1)} %bitcast.94) | data formatting | bytes 266240 | tf_op jit(solution)/shard_map/reshape | solution.py:88
  46.2 5.8 %all-to-all-start.1 = ((bf16[32,2,1040]{2,1,0:T(2,128)(2,1)}), bf16[32,2,1040]{2,1,0:T(2,128)(2,1)S(1)}, u32[]{:S(2)}, u32[]{:S(2)}) async-start(bf16[32,2,1040]{2,1,0:T(2,128)(2,1)} %copy.80), calls=%async_computation.1 | async-start | bytes 294912 | tf_op jit(solution)/shard_map/all_to_all | solution.py:89
  52.1 1.5 %maximum_bitcast_fusion = (bf16[1,64,20,256]{3,1,0,2:T(8,128)(2,1)S(1)}, bf16[1,64,20,256]{3,1,0,2:T(8,128)(2,1)S(1)}) fusion(bf16[64,20,128]{2,0,1:T(8,128)(2,1)} %get-tuple-element.36, bf16[64,20,128]{2,0,1:T(8,128)(2,1)} %get-tuple-element.38, bf16[64,20,128]{2,0,1:T(8,128)(2,1)} %get-tuple-element.37), kind=kLoop, calls=%fused_computation.23 | loop fusion | flops 2621440 | bytes 2293760 | tf_op jit(solution)/shard_map/stack | solution.py:37
  53.5 0.8 %copy-done.1 = bf16[1,64,20,256]{3,1,0,2:T(8,128)(2,1)} copy-done((bf16[1,64,20,256]{3,1,0,2:T(8,128)(2,1)}, bf16[1,64,20,256]{3,1,0,2:T(8,128)(2,1)S(1)}, u32[]{:S(2)}) %copy-start.1) | copy-done | bytes 655384
  54.6 0.9 %fusion.25 = bf16[2,32,20,256]{3,1,0,2:T(8,128)(2,1)} fusion(bf16[1,64,20,256]{3,1,0,2:T(8,128)(2,1)S(1)} %get-tuple-element.34, bf16[1,64,20,256]{3,1,0,2:T(8,128)(2,1)S(1)} %get-tuple-element.35), kind=kLoop, calls=%fused_computation.22 | loop fusion | flops 327680 | bytes 1966080 | tf_op jit(solution)/shard_map/stack | solution.py:37
  55.5 4.9 %all-to-all-done.1 = bf16[32,2,1040]{2,1,0:T(2,128)(2,1)S(1)} async-done(((bf16[32,2,1040]{2,1,0:T(2,128)(2,1)}), bf16[32,2,1040]{2,1,0:T(2,128)(2,1)S(1)}, u32[]{:S(2)}, u32[]{:S(2)}) %all-to-all-start.1) | async-done | bytes 133152 | tf_op jit(solution)/shard_map/all_to_all | solution.py:89
  60.5 1.1 %copy.81 = bf16[32,2,1040]{0,2,1:T(8,128)(2,1)} copy(bf16[32,2,1040]{2,1,0:T(2,128)(2,1)S(1)} %all-to-all-done.1) | data formatting | bytes 266240 | tf_op jit(solution)/shard_map/all_to_all | solution.py:89
  61.6 1.1 %copy.111 = bf16[32,1,2,65,16]{0,4,2,3,1:T(8,128)(2,1)S(1)} copy(bf16[32,1,2,65,16]{0,4,3,2,1:T(8,128)(2,1)} %bitcast.95) | data formatting | bytes 266240 | tf_op jit(solution)/shard_map/reshape | solution.py:90
  64.7 1.3 %copy.83 = bf16[1,2,32,40,16]{3,2,4,1,0:T(8,128)(2,1)S(1)} copy(bf16[1,2,32,40,16]{2,4,1,3,0:T(8,128)(2,1)} %slice.72) | data formatting | bytes 163840 | tf_op jit(solution)/shard_map/slice | solution.py:96
  66.1 1.1 %reshape.266 = bf16[1,2,64,20,16]{3,2,4,1,0:T(8,128)(2,1)} reshape(bf16[1,2,32,40,16]{3,2,4,1,0:T(8,128)(2,1)S(1)} %copy.83) | data formatting | bytes 163840 | tf_op jit(solution)/shard_map/reshape | solution.py:94
  67.1 2.0 %copy.85 = bf16[1,2,64,20,16]{2,4,1,3,0:T(8,128)(2,1)} copy(bf16[1,2,64,20,16]{3,2,4,1,0:T(8,128)(2,1)} %reshape.266) | data formatting | bytes 163840 | tf_op jit(solution)/shard_map/reshape | solution.py:94
  69.2 0.9 %copy.84 = bf16[1,2,32,5,16]{4,1,3,2,0:T(2,128)(2,1)S(1)} copy(bf16[1,2,32,5,16]{2,4,1,3,0:T(8,128)(2,1)} %slice.74) | data formatting | bytes 20480 | tf_op jit(solution)/shard_map/slice | solution.py:98
  70.2 2.9 %fusion.16 = f32[1,16,20,256]{3,1,2,0:T(8,128)} fusion(bf16[1,64,20,256]{3,1,0,2:T(8,128)(2,1)} %copy-done.2, bf16[1,64,20,256]{3,1,0,2:T(8,128)(2,1)} %copy-done.1, bf16[2,32,20,256]{3,1,0,2:T(8,128)(2,1)} %fusion.25, bf16[1,2,8,20,16]{2,4,1,3,0:T(8,128)(2,1)S(1)} %copy.86, bf16[1,2,32,20,16]{2,4,1,3,0:T(8,128)(2,1)} %slice.73, ...), kind=kOutput, calls=%fused_computation.12 | convolution fusion | flops 45127680 | bytes 2426880 | tf_op jit(solution)/shard_map/rchqe,chqx->reqx/dot_general | solution.py:105
  73.2 1.9 %reshape.268 = f32[16,20,2,128]{3,2,0,1:T(2,128)} reshape(f32[1,16,20,256]{3,1,2,0:T(8,128)} %fusion.16) | data formatting | bytes 655360 | tf_op jit(solution)/shard_map/reshape.4
  75.0 1.5 %fusion.20 = f32[16,1,20,128]{3,2,0,1:T(8,128)S(1)} fusion(f32[16,20,2,128]{3,2,0,1:T(2,128)} %reshape.268, f32[20,1,20]{0,2,1:T(8,128)S(1)} %get-tuple-element.53, f32[20,1,20]{0,2,1:T(8,128)S(1)} %copy-done.7), kind=kOutput, calls=%fused_computation.16 | convolution fusion | flops 19661600 | bytes 494720 | tf_op jit(solution)/shard_map/reqxl,qxh->erhl/dot_general | solution.py:113
  76.5 0.8 %tanh.24 = f32[16,1,2560]{2,1,0:T(1,128)} reshape(f32[16,1,20,128]{3,2,0,1:T(8,128)S(1)} %fusion.20) | data formatting | bytes 327680 | tf_op jit(solution)/shard_map/tanh | solution.py:114
  (41 shorter events, 7.7 us)
Async XLA Ops:
  0.6 28.0 %copy-start = (bf16[40,32,1280]{2,1,0:T(8,128)(2,1)S(1)}, bf16[40,32,1280]{2,1,0:T(8,128)(2,1)}, u32[]{:S(2)}) copy-start(bf16[40,32,1280]{2,1,0:T(8,128)(2,1)} %param.19) | copy-start | bytes 9830404
  8.7 28.9 %all-to-all-start = ((bf16[32,3,800]{2,1,0:T(4,128)(2,1)}), bf16[32,3,800]{2,1,0:T(4,128)(2,1)S(1)}, u32[]{:S(2)}, u32[]{:S(2)}) async-start(bf16[32,3,800]{2,1,0:T(4,128)(2,1)} %copy.75), calls=%async_computation | async-start | bytes 458752 | tf_op jit(solution)/shard_map/all_to_all | solution.py:71
  28.6 2.1 %copy-start.5 = (f32[64,128]{1,0:T(8,128)S(1)}, f32[64,128]{1,0:T(8,128)}, u32[]{:S(2)}) copy-start(f32[64,128]{1,0:T(8,128)} %get-tuple-element.40) | copy-start | bytes 98308
  28.6 2.1 %copy-start.6 = (f32[20,128]{1,0:T(8,128)S(1)}, f32[20,128]{1,0:T(8,128)}, u32[]{:S(2)}) copy-start(f32[20,128]{1,0:T(8,128)} %get-tuple-element.42) | copy-start | bytes 30724
  28.6 3.4 %copy-start.3 = (f32[16,2,20,640]{3,1,2,0:T(2,128)S(1)}, f32[16,2,20,640]{3,1,2,0:T(2,128)}, u32[]{:S(2)}) copy-start(f32[16,2,20,640]{3,1,2,0:T(2,128)} %param.13) | copy-start | bytes 4915204
  28.6 3.4 %copy-start.4 = (bf16[16,2,20,640]{3,1,2,0:T(2,128)(2,1)S(1)}, bf16[16,2,20,640]{3,1,2,0:T(2,128)(2,1)}, u32[]{:S(2)}) copy-start(bf16[16,2,20,640]{3,1,2,0:T(2,128)(2,1)} %param.14) | copy-start | bytes 2457604
  30.7 5.8 %copy-start.8 = (bf16[20,32,640]{2,1,0:T(8,128)(2,1)S(1)}, bf16[20,32,640]{2,1,0:T(8,128)(2,1)}, u32[]{:S(2)}) copy-start(bf16[20,32,640]{2,1,0:T(8,128)(2,1)} %param.20) | copy-start | bytes 2457604
  46.2 14.3 %all-to-all-start.1 = ((bf16[32,2,1040]{2,1,0:T(2,128)(2,1)}), bf16[32,2,1040]{2,1,0:T(2,128)(2,1)S(1)}, u32[]{:S(2)}, u32[]{:S(2)}) async-start(bf16[32,2,1040]{2,1,0:T(2,128)(2,1)} %copy.80), calls=%async_computation.1 | async-start | bytes 294912 | tf_op jit(solution)/shard_map/all_to_all | solution.py:89
  53.5 0.9 %copy-start.1 = (bf16[1,64,20,256]{3,1,0,2:T(8,128)(2,1)}, bf16[1,64,20,256]{3,1,0,2:T(8,128)(2,1)S(1)}, u32[]{:S(2)}) copy-start(bf16[1,64,20,256]{3,1,0,2:T(8,128)(2,1)S(1)} %get-tuple-element.34) | copy-start | bytes 1966084
  53.5 1.1 %copy-start.2 = (bf16[1,64,20,256]{3,1,0,2:T(8,128)(2,1)}, bf16[1,64,20,256]{3,1,0,2:T(8,128)(2,1)S(1)}, u32[]{:S(2)}) copy-start(bf16[1,64,20,256]{3,1,0,2:T(8,128)(2,1)S(1)} %get-tuple-element.35) | copy-start | bytes 1966084
  70.2 4.8 %copy-start.7 = (f32[20,1,20]{0,2,1:T(8,128)S(1)}, f32[20,1,20]{0,2,1:T(8,128)}, u32[]{:S(2)}) copy-start(f32[20,1,20]{0,2,1:T(8,128)} %get-tuple-element.54) | copy-start | bytes 4804

commit v2 on v0

v2 whole, which is shorter than its diff:
```python
import functools
import math

import jax
import jax.numpy as jnp
from jax import lax
from jax.experimental import pallas as pl
from jax.experimental.pallas import tpu as pltpu
from jax.sharding import PartitionSpec as P

NLON = 2560
LANES = 128
FOLD = NLON // LANES


def advance(state, noise, decay_rate, amp_rate, offset):
    slots = state.shape[3]
    mode_ids = offset + jnp.arange(state.shape[2], dtype=jnp.int32)
    degree_ids = jnp.arange(slots, dtype=jnp.int32)
    inside = mode_ids[:, None] + degree_ids[None, :] < slots
    updated = decay_rate * state + amp_rate * noise.astype(jnp.float32)
    return jnp.where(inside, updated, jnp.zeros_like(updated))


def phase_rows(block, devices):
    return max((p * block % FOLD + block - 1) // FOLD + 1 for p in range(devices))


def phase_blocks(fourier, place, devices, modes=None):
    rows, parts, block, members = fourier.shape
    high = phase_rows(block, devices)
    if block % FOLD:
        start = (place * block % FOLD).astype(jnp.int32)
        room = jnp.zeros((rows, parts, high * FOLD, members), fourier.dtype)
        zero = jnp.zeros((), jnp.int32)
        fourier = lax.dynamic_update_slice(room, fourier, (zero, zero, start, zero))
    return fourier.reshape(rows, parts * high, FOLD * members)


def base_phases(blocks, devices, width):
    source = jnp.arange(devices, dtype=jnp.int32)[:, None]
    cols, parts = [], []
    for block in blocks:
        for part in range(2):
            for j in range(phase_rows(block, devices)):
                cols.append(source * block // FOLD + j)
                parts.append(part)
    while len(cols) < width:
        cols.append(source * 0)
        parts.append(0)
    high = jnp.concatenate(cols, axis=1).reshape(-1, 1)
    part = jnp.tile(jnp.array(parts, jnp.int32), devices)[:, None]
    lon = jnp.arange(LANES, dtype=jnp.int32)[None, :]
    turns = (high * lon + part * (LANES // 4)) % LANES
    angle = turns.astype(jnp.float32) * (2.0 * math.pi / LANES)
    first = jnp.where(high == 0, 0.5, 1.0).astype(jnp.float32) * jnp.ones_like(angle)
    low = (jnp.arange(FOLD, dtype=jnp.int32)[:, None] * lon).astype(jnp.float32) * (
        2.0 * math.pi / NLON
    )
    return (
        jnp.stack([2.0 * jnp.cos(angle), 2.0 * jnp.sin(angle), first]),
        jnp.stack([jnp.cos(low), jnp.sin(low)]),
    )


def longitude_kernel(members, got_ref, base_ref, low_ref, out_ref):
    own = got_ref.shape[1]
    for i in range(own):
        spread = got_ref[:, i].astype(jnp.float32)
        spread = spread.reshape(spread.shape[0] * spread.shape[1], spread.shape[2])
        lanes = -spread.shape[1] % LANES
        if lanes:
            spread = jnp.concatenate(
                [spread, jnp.zeros((spread.shape[0], lanes), jnp.float32)], axis=1
            )
        turned = spread.T.astype(jnp.bfloat16)
        totals = [None] * FOLD
        for q in range(FOLD):
            re, im = base_ref[0], base_ref[1]
            if q == 0:
                re, im = re * base_ref[2], im * base_ref[2]
            cl, sl = low_ref[0, q : q + 1], low_ref[1, q : q + 1]
            table = jnp.concatenate([re * cl - im * sl, im * cl + re * sl], axis=1)
            part = jnp.dot(
                turned[q * members : (q + 1) * members],
                table.astype(jnp.bfloat16),
                preferred_element_type=jnp.float32,
            )
            real, imag = part[:, :LANES], part[:, LANES:]
            for h in range(FOLD):
                turn = 2.0 * math.pi * (q * h % FOLD) / FOLD
                term = math.cos(turn) * real - math.sin(turn) * imag
                totals[h] = term if q == 0 else totals[h] + term
        for h in range(FOLD):
            out_ref[:, i, h * LANES : (h + 1) * LANES] = jnp.tanh(totals[h])


def coarse_kernel(
    part_modes, decay_ref, amp_ref, state_ref, noise_ref, basis_ref, next_ref, mixed_ref
):
    held, parts, modes, slots = state_ref.shape
    mode_ids = lax.broadcasted_iota(jnp.int32, (modes, slots), 0)
    degree_ids = lax.broadcasted_iota(jnp.int32, (modes, slots), 1)
    inside = mode_ids + degree_ids < slots
    planes = []
    for e in range(held):
        for c in range(parts):
            new = decay_ref[2] * state_ref[e, c] + amp_ref[2] * noise_ref[e, c].astype(jnp.float32)
            new = jnp.where(inside, new, 0.0)
            next_ref[e, c] = new
            planes.append(new)
    for r in range(basis_ref.shape[0]):
        planes.append(basis_ref[r].astype(jnp.float32))
    empty = jnp.zeros((part_modes, slots), jnp.float32)
    for d in range(mixed_ref.shape[0]):
        pieces = []
        for plane in planes:
            piece = plane[d * part_modes : min((d + 1) * part_modes, modes)]
            missing = part_modes - piece.shape[0]
            if missing == part_modes:
                piece = empty
            elif missing:
                piece = jnp.concatenate([piece, empty[:missing]], axis=0)
            pieces.append(piece)
        mixed_ref[d] = jnp.concatenate(pieces, axis=0).astype(jnp.bfloat16)


def body(
    fine_state,
    fine_noise,
    medium_state,
    medium_noise,
    coarse_state,
    coarse_noise,
    decay,
    amplitude,
    fine_basis,
    medium_basis,
    coarse_basis,
):
    devices = lax.axis_size("scale") * lax.axis_size("lat")
    lat = lax.axis_size("lat")
    held, _, modes, slots = coarse_state.shape
    own = coarse_basis.shape[0]
    part_modes = -(-modes // devices)
    vmem = pl.BlockSpec(memory_space=pltpu.VMEM)
    smem = pl.BlockSpec(memory_space=pltpu.SMEM)
    coarse_next, mixed = pl.pallas_call(
        functools.partial(coarse_kernel, part_modes),
        out_shape=(
            jax.ShapeDtypeStruct(coarse_state.shape, jnp.float32),
            jax.ShapeDtypeStruct((devices, (2 * held + own) * part_modes, slots), jnp.bfloat16),
        ),
        in_specs=[smem, smem, vmem, vmem, vmem],
        out_specs=(vmem, vmem),
    )(decay, amplitude, coarse_state, coarse_noise, coarse_basis)
    mixed = lax.all_to_all(mixed, ("scale", "lat"), split_axis=0, concat_axis=0, tiled=True)
    mixed = mixed.reshape(devices, 2 * held + own, part_modes, slots)
    coarse_half = mixed[:lat, : 2 * held].reshape(lat * held, 2, part_modes, slots)
    coarse_rows = mixed[:, 2 * held :].reshape(devices * own, part_modes, slots)
    place = lax.axis_index(("scale", "lat"))
    fine_next = advance(fine_state, fine_noise, decay[0], amplitude[0], place * fine_state.shape[2])
    medium_next = advance(
        medium_state, medium_noise, decay[1], amplitude[1], place * medium_state.shape[2]
    )
    fourier = []
    for half, basis, form in (
        (fine_next.astype(jnp.bfloat16), fine_basis, "ecmk,mrk->rcme"),
        (medium_next.astype(jnp.bfloat16), medium_basis, "ecmk,mrk->rcme"),
        (coarse_half, coarse_rows, "ecmk,rmk->rcme"),
    ):
        fourier.append(
            jnp.einsum(form, half, basis, preferred_element_type=jnp.float32).astype(jnp.bfloat16)
        )
    members = coarse_half.shape[0]
    blocks = [x.shape[2] for x in fourier]
    both = jnp.concatenate([phase_blocks(x, place, devices) for x in fourier], axis=1)
    width = -(-both.shape[1] // 8) * 8
    both = jnp.pad(both, ((0, 0), (0, width - both.shape[1]), (0, 0)))
    got = lax.all_to_all(both, ("scale", "lat"), split_axis=0, concat_axis=0, tiled=True)
    got = got.reshape(devices, own, width, FOLD * members)
    base, low = base_phases(blocks, devices, width)
    pattern = pl.pallas_call(
        functools.partial(longitude_kernel, members),
        out_shape=jax.ShapeDtypeStruct((members, own, NLON), jnp.float32),
        in_specs=[vmem, vmem, vmem],
        out_specs=vmem,
    )(got, base, low)
    return (fine_next, medium_next, coarse_next, pattern)


def solution(mesh):
    return jax.shard_map(
        body,
        mesh=mesh,
        in_specs=(
            P(None, None, ("scale", "lat"), None),
            P(None, None, ("scale", "lat"), None),
            P(None, None, ("scale", "lat"), None),
            P(None, None, ("scale", "lat"), None),
            P("lat", None, None, None),
            P("lat", None, None, None),
            P(),
            P(),
            P(("scale", "lat"), None, None),
            P(("scale", "lat"), None, None),
            P(("scale", "lat"), None, None),
        ),
        out_specs=(
            P(None, None, ("scale", "lat"), None),
            P(None, None, ("scale", "lat"), None),
            P("lat", None, None, None),
            P(None, ("scale", "lat"), None),
        ),
        check_vma=False,
    )
```

time: 171 us -> 62.7 us (0.37)
  other arithmetic: 107 us -> 23.2 us
  matrix products: 21.8 us -> 1.84 us
  between operations: 14.3 us -> 0.75 us
  waiting for transfers between devices: 0.52 us -> 6.43 us
  Pallas kernels: 0 us -> 4.77 us
    another operation x3 -> x2, other arithmetic: 92.4 us -> 3.07 us  [the longest x1 1.74 us: base_phases(): jnp.stack([2.0 * jnp.cos(angle), 2.0 * jnp.sin(angle), first])]
    dot_general x6 -> x3, matrix products: 21.8 us -> 1.84 us  [body(): jnp.einsum(form, half, basis, preferred_element_type=jnp.float32)]
    all_to_all x2, waiting for transfers between devices: 0.5 us -> 6.43 us  [the longest x1 6.42 us: body(): lax.all_to_all(both, ('scale', 'lat'), split_axis=0, concat_axis=0, tiled...]
    pallas_call x0 -> x2, Pallas kernels: none -> 4.77 us  [the longest x1 2.69 us: body(): pl.pallas_call(functools.partial(longitude_kernel, members), out_shape=ja...]
    unnamed x17 -> x6, local copies, waits for them, and re-layouts: 5.27 us -> 0.68 us
    convert_element_type x1, other arithmetic: 5.5 us -> 9.22 us  [body(): fine_next.astype(jnp.bfloat16)]
    convert_element_type x1 -> x0, other arithmetic: 3.1 us -> none  [body(): coarse_half = coarse_next.astype(jnp.bfloat16)]
    reshape x1 -> x3, local copies, waits for them, and re-layouts: 0.95 us -> 3.56 us  [phase_blocks(): return fourier.reshape(rows, parts * high, FOLD * members)]
  transfers between devices with their start and end apart: 3 -> 2, of which waited for: 1 -> 1; matrix products, arithmetic and copies ran while one was open for 72% -> 55% of each run, Pallas kernels for 0% -> 0%
where the time goes in v2:
time: 62.7 us; the launch traced here: 62 us
  other arithmetic  23.2 us (37%)
  starting transfers between devices  13.2 us (21%)
  local copies, waits for them, and re-layouts  11.9 us (19%)
  waiting for transfers between devices  6.43 us (10%)
  Pallas kernels  4.77 us (8%)
  matrix products  1.84 us (3%)
  between operations  0.75 us (1%)
    convert_element_type x1, other arithmetic, body(): fine_next.astype(jnp.bfloat16)  9.22 us
    all_to_all x1, starting transfers between devices, body(): lax.all_to_all(mixed, ('scale', 'lat'), split_axis=0, concat_axis=0, tile...  7.33 us
    all_to_all x1, waiting for transfers between devices, body(): lax.all_to_all(both, ('scale', 'lat'), split_axis=0, concat_axis=0, tiled...  6.42 us
    all_to_all x1, starting transfers between devices, body(): lax.all_to_all(both, ('scale', 'lat'), split_axis=0, concat_axis=0, tiled...  5.83 us
    convert_element_type x1, other arithmetic, body(): medium_next.astype(jnp.bfloat16)  5.52 us
    reshape x3, local copies, waits for them, and re-layouts, phase_blocks(): return fourier.reshape(rows, parts * high, FOLD * members)  3.56 us
    pallas_call x1, Pallas kernels, body(): pl.pallas_call(functools.partial(longitude_kernel, members), out_shape=ja...  2.69 us
    pallas_call x1, Pallas kernels, body(): pl.pallas_call(functools.partial(coarse_kernel, part_modes), out_shape=(j...  2.08 us
  transfers between devices with their start and end apart: 2, of which 1 were waited for; matrix products, arithmetic and copies ran while one was open for 55% of the time, Pallas kernels for 0%

profile of v2, /device:TPU:0, one launch (start us, length us, event | category | flops | bytes accessed | tf_op | source)
XLA Modules:
  0.0 62.0 jit_solution(7280796774243763467)
XLA Ops:
  0.6 2.1 %shard_map.147 = (f32[1,2,160,160]{3,2,1,0:T(8,128)}, bf16[32,15,160]{2,1,0:T(8,128)(2,1)}) custom-call(f32[3]{0:T(128)} %decay_ref.1, f32[3]{0:T(128)} %amp_ref.1, f32[1,2,160,160]{3,2,1,0:T(8,128)} %state_ref.1, bf16[1,2,160,160]{3,2,1,0:T(8,128)(2,1)} %noise_ref.1, bf16[1,160,160]{2,1,0:T(8,128)(2,1)} %basis_ref.1), custom_call_target="tpu_custom_call" | custom-call | tf_op jit(solution)/shard_map/pallas_call | solution.py:148
  2.7 7.3 %all-to-all-start = ((bf16[32,15,160]{2,1,0:T(8,128)(2,1)}), bf16[32,15,160]{2,1,0:T(8,128)(2,1)S(1)}, u32[]{:S(2)}, u32[]{:S(2)}) async-start(bf16[32,15,160]{2,1,0:T(8,128)(2,1)} %get-tuple-element.7), calls=%async_computation | async-start | bytes 524288 | tf_op jit(solution)/shard_map/all_to_all | solution.py:157
  10.1 1.3 %fusion.25 = (f32[1]{0:T(128)}, f32[1]{0:T(128)}) fusion(f32[3]{0:T(128)} %decay_ref.1), kind=kLoop, calls=%fused_computation.41 | loop fusion | bytes 16 | tf_op jit(solution)/shard_map/slice | solution.py:164
  11.4 1.3 %fusion.26 = (f32[1]{0:T(128)}, f32[1]{0:T(128)}) fusion(f32[3]{0:T(128)} %amp_ref.1), kind=kLoop, calls=%fused_computation.42 | loop fusion | bytes 16 | tf_op jit(solution)/shard_map/slice | solution.py:164
  12.8 0.7 %fusion.21 = (f32[1,20,128]{2,1,0:T(8,128)}, f32[1,20,128]{2,1,0:T(8,128)}) fusion(), kind=kLoop, calls=%fused_computation.30 | loop fusion | flops 7680 | bytes 20480 | tf_op jit(solution)/shard_map/sin | solution.py:62
  13.4 0.1 add_compare_fusion
  13.5 9.2 %fusion.23 = (bf16[16,2,40,1280]{3,2,1,0:T(8,128)(2,1)S(1)}, f32[16,2,40,1280]{3,2,1,0:T(8,128)}) fusion(bf16[16,2,40,1280]{3,2,1,0:T(8,128)(2,1)} %param.13, f32[]{:T(128)} %bitcast.1, f32[16,2,40,1280]{3,2,1,0:T(8,128)} %param.12, f32[]{:T(128)} %bitcast, pred[40,1280]{1,0:T(8,128)(4,1)S(1)} %add_compare_fusion), kind=kLoop, calls=%fused_computation.39 | loop fusion | flops 9830400 | bytes 19712008 | tf_op jit(solution)/shard_map/convert_element_type | solution.py:168
  22.8 1.3 %fusion.8 = bf16[32,2,40,16]{0,3,1,2:T(8,128)(2,1)S(1)} fusion(bf16[40,32,1280]{2,1,0:T(8,128)(2,1)S(1)} %copy-done, bf16[16,2,40,1280]{3,2,1,0:T(8,128)(2,1)S(1)} %get-tuple-element.8), kind=kOutput, calls=%fused_computation.6 | convolution fusion | flops 104898560 | bytes 6635520 | tf_op jit(solution)/shard_map/ecmk,mrk->rcme/dot_general | solution.py:173
  24.1 0.8 %copy.34 = bf16[32,2,40,16]{0,3,2,1:T(8,128)(2,1)} copy(bf16[32,2,40,16]{0,3,1,2:T(8,128)(2,1)S(1)} %fusion.8) | data formatting | bytes 163840 | tf_op jit(solution)/shard_map/convert_element_type | solution.py:173
  24.8 1.8 %copy.40 = bf16[32,4,320]{2,1,0:T(4,128)(2,1)} copy(bf16[32,4,320]{0,2,1:T(8,128)(2,1)} %bitcast.35) | data formatting | bytes 163840 | tf_op jit(solution)/shard_map/reshape | solution.py:37
  26.6 0.1 add_compare_fusion.1
  26.7 5.5 %fusion.24 = (bf16[16,2,20,640]{3,1,2,0:T(2,128)(2,1)S(1)}, f32[16,2,20,640]{3,1,2,0:T(2,128)}) fusion(bf16[16,2,20,640]{3,1,2,0:T(2,128)(2,1)} %param.15, f32[]{:T(128)} %bitcast.3, f32[16,2,20,640]{3,1,2,0:T(2,128)} %param.14, f32[]{:T(128)} %bitcast.2, pred[20,640]{1,0:T(8,128)(4,1)S(1)} %add_compare_fusion.1), kind=kLoop, calls=%fused_computation.40 | loop fusion | flops 2457600 | bytes 4928008 | tf_op jit(solution)/shard_map/convert_element_type | solution.py:169
  32.2 0.4 fusion.13
  32.6 0.7 %copy.36 = bf16[32,2,20,16]{0,3,2,1:T(8,128)(2,1)} copy(bf16[32,2,20,16]{0,3,1,2:T(8,128)(2,1)S(1)} %fusion.13) | data formatting | bytes 81920 | tf_op jit(solution)/shard_map/convert_element_type | solution.py:173
  33.3 1.7 %copy.41 = bf16[32,2,320]{2,1,0:T(2,128)(2,1)} copy(bf16[32,2,320]{0,2,1:T(8,128)(2,1)} %bitcast.38) | data formatting | bytes 81920 | tf_op jit(solution)/shard_map/reshape | solution.py:37
  34.9 0.6 concatenate.7
  35.6 0.8 %copy.43 = s32[32,8]{1,0:T(8,128)S(1)} copy(s32[32,8]{0,1:T(8,128)} %concatenate.7) | data formatting | bytes 2048 | tf_op jit(solution)/shard_map/concatenate | solution.py:51
  36.3 0.7 %mul.233 = s32[256]{0:T(256)} reshape(s32[32,8]{1,0:T(8,128)S(1)} %copy.43) | data formatting | bytes 2048 | tf_op jit(solution)/shard_map/mul | solution.py:54
  37.0 0.7 %tile.2 = s32[32,8]{1,0:T(8,128)S(1)} broadcast(s32[8]{0:T(128)} %constant.102), dimensions={1} | broadcast | bytes 1056 | tf_op jit(solution)/shard_map/tile | solution.py:52
  37.7 0.6 %mul.239 = s32[256]{0:T(256)} reshape(s32[32,8]{1,0:T(8,128)S(1)} %tile.2) | data formatting | bytes 2048 | tf_op jit(solution)/shard_map/mul | solution.py:54
  38.3 1.3 %pad_maximum_fusion.2.low_ref = f32[2,20,128]{2,1,0:T(8,128)} fusion(f32[1,20,128]{2,1,0:T(8,128)} %get-tuple-element.22, f32[1,20,128]{2,1,0:T(8,128)} %get-tuple-element.23), kind=kLoop, calls=%fused_computation.28 | loop fusion | flops 5120 | bytes 40960 | tf_op jit(solution)/shard_map/stack | solution.py:62
  39.6 2.0 %cosine_multiply_fusion = (f32[1,256,128]{2,1,0:T(8,128)}, f32[1,256,128]{2,1,0:T(8,128)}) fusion(s32[256]{0:T(256)} %mul.239, s32[256]{0:T(256)} %mul.233), kind=kLoop, calls=%fused_computation.23 | loop fusion | flops 557056 | bytes 264192 | tf_op jit(solution)/shard_map/mul | solution.py:61
  41.7 0.1 fusion.14
  41.9 0.1 copy.42
  42.1 1.8 %pad_maximum_fusion.1 = bf16[32,8,320]{2,1,0:T(8,128)(2,1)} fusion(bf16[32,2,320]{2,1,0:T(2,128)(2,1)S(1)} %copy.42, bf16[32,2,320]{2,1,0:T(2,128)(2,1)} %copy.41, bf16[32,4,320]{2,1,0:T(4,128)(2,1)} %copy.40), kind=kLoop, calls=%fused_computation.15 | loop fusion | flops 491520 | bytes 327680 | tf_op jit(solution)/shard_map/concatenate | solution.py:177
  43.8 5.8 %all-to-all-start.1 = ((bf16[32,8,320]{2,1,0:T(8,128)(2,1)}), bf16[32,8,320]{2,1,0:T(8,128)(2,1)S(1)}, u32[]{:S(2)}, u32[]{:S(2)}) async-start(bf16[32,8,320]{2,1,0:T(8,128)(2,1)} %pad_maximum_fusion.1), calls=%async_computation.1 | async-start | bytes 393216 | tf_op jit(solution)/shard_map/all_to_all | solution.py:180
  49.7 0.7 %compare_select_fusion = f32[256]{0:T(256)S(1)} fusion(s32[256]{0:T(256)} %mul.233), kind=kLoop, calls=%fused_computation.32 | loop fusion | flops 512 | bytes 2048 | tf_op jit(solution)/shard_map/jit(_where)/select_n | solution.py:56
  50.3 0.1 stack.6
  50.4 1.7 %pad_maximum_fusion.base_ref = f32[3,256,128]{2,1,0:T(8,128)} fusion(f32[1,256,128]{2,1,0:T(8,128)S(1)} %stack.6, f32[1,256,128]{2,1,0:T(8,128)} %get-tuple-element.13, f32[1,256,128]{2,1,0:T(8,128)} %get-tuple-element.12), kind=kLoop, calls=%fused_computation.13 | loop fusion | flops 196608 | bytes 786432 | tf_op jit(solution)/shard_map/stack | solution.py:61
  52.2 6.4 %all-to-all-done.1 = bf16[32,8,320]{2,1,0:T(8,128)(2,1)S(1)} async-done(((bf16[32,8,320]{2,1,0:T(8,128)(2,1)}), bf16[32,8,320]{2,1,0:T(8,128)(2,1)S(1)}, u32[]{:S(2)}, u32[]{:S(2)}) %all-to-all-start.1) | async-done | bytes 163872 | tf_op jit(solution)/shard_map/all_to_all | solution.py:180
  58.6 0.7 %copy-done.1 = bf16[32,8,320]{2,1,0:T(8,128)(2,1)} copy-done((bf16[32,8,320]{2,1,0:T(8,128)(2,1)}, bf16[32,8,320]{2,1,0:T(8,128)(2,1)S(1)}, u32[]{:S(2)}) %copy-start.1) | copy-done | bytes 163864
  59.3 2.7 %shard_map.148 = f32[16,1,2560]{2,1,0:T(1,128)} custom-call(bf16[32,1,8,320]{3,2,1,0:T(8,128)(2,1)} %bitcast.36, f32[3,256,128]{2,1,0:T(8,128)} %pad_maximum_fusion.base_ref, f32[2,20,128]{2,1,0:T(8,128)} %pad_maximum_fusion.2.low_ref), custom_call_target="tpu_custom_call" | custom-call | tf_op jit(solution)/shard_map/pallas_call | solution.py:183
  (13 shorter events, 0.2 us)
Async XLA Ops:
  0.6 22.1 %copy-start = (bf16[40,32,1280]{2,1,0:T(8,128)(2,1)S(1)}, bf16[40,32,1280]{2,1,0:T(8,128)(2,1)}, u32[]{:S(2)}) copy-start(bf16[40,32,1280]{2,1,0:T(8,128)(2,1)} %param.20) | copy-start | bytes 9830404
  2.7 38.9 %all-to-all-start = ((bf16[32,15,160]{2,1,0:T(8,128)(2,1)}), bf16[32,15,160]{2,1,0:T(8,128)(2,1)S(1)}, u32[]{:S(2)}, u32[]{:S(2)}) async-start(bf16[32,15,160]{2,1,0:T(8,128)(2,1)} %get-tuple-element.7), calls=%async_computation | async-start | bytes 524288 | tf_op jit(solution)/shard_map/all_to_all | solution.py:157
  26.6 5.6 %copy-start.2 = (bf16[20,32,640]{2,1,0:T(8,128)(2,1)S(1)}, bf16[20,32,640]{2,1,0:T(8,128)(2,1)}, u32[]{:S(2)}) copy-start(bf16[20,32,640]{2,1,0:T(8,128)(2,1)} %param.21) | copy-start | bytes 2457604
  43.8 14.8 %all-to-all-start.1 = ((bf16[32,8,320]{2,1,0:T(8,128)(2,1)}), bf16[32,8,320]{2,1,0:T(8,128)(2,1)S(1)}, u32[]{:S(2)}, u32[]{:S(2)}) async-start(bf16[32,8,320]{2,1,0:T(8,128)(2,1)} %pad_maximum_fusion.1), calls=%async_computation.1 | async-start | bytes 393216 | tf_op jit(solution)/shard_map/all_to_all | solution.py:180
  58.6 0.7 %copy-start.1 = (bf16[32,8,320]{2,1,0:T(8,128)(2,1)}, bf16[32,8,320]{2,1,0:T(8,128)(2,1)S(1)}, u32[]{:S(2)}) copy-start(bf16[32,8,320]{2,1,0:T(8,128)(2,1)S(1)} %all-to-all-done.1) | copy-start | bytes 491524

commit v3 on v2

--- a/solution.py
+++ b/solution.py
@@ -3,6 +3,7 @@
 
 import jax
 import jax.numpy as jnp
+import numpy as np
 from jax import lax
 from jax.experimental import pallas as pl
 from jax.experimental.pallas import tpu as pltpu
@@ -37,8 +38,8 @@
     return fourier.reshape(rows, parts * high, FOLD * members)
 
 
-def base_phases(blocks, devices, width):
-    source = jnp.arange(devices, dtype=jnp.int32)[:, None]
+def received_rows(blocks, devices, width):
+    source = np.arange(devices, dtype=np.int32)
     cols, parts = [], []
     for block in blocks:
         for part in range(2):
@@ -48,22 +49,33 @@
     while len(cols) < width:
         cols.append(source * 0)
         parts.append(0)
-    high = jnp.concatenate(cols, axis=1).reshape(-1, 1)
-    part = jnp.tile(jnp.array(parts, jnp.int32), devices)[:, None]
-    lon = jnp.arange(LANES, dtype=jnp.int32)[None, :]
+    high = np.stack(cols, axis=1).reshape(-1, 1)
+    part = np.tile(np.array(parts, np.int32), devices)[:, None]
+    return np.concatenate([high, part], axis=1).astype(np.int32)
+
+
+def table_kernel(rows_ref, table_ref):
+    count = rows_ref.shape[0]
+    high, part = rows_ref[:, 0:1], rows_ref[:, 1:2]
+    lon = lax.broadcasted_iota(jnp.int32, (count, LANES), 1)
     turns = (high * lon + part * (LANES // 4)) % LANES
     angle = turns.astype(jnp.float32) * (2.0 * math.pi / LANES)
-    first = jnp.where(high == 0, 0.5, 1.0).astype(jnp.float32) * jnp.ones_like(angle)
-    low = (jnp.arange(FOLD, dtype=jnp.int32)[:, None] * lon).astype(jnp.float32) * (
-        2.0 * math.pi / NLON
-    )
-    return (
-        jnp.stack([2.0 * jnp.cos(angle), 2.0 * jnp.sin(angle), first]),
-        jnp.stack([jnp.cos(low), jnp.sin(low)]),
-    )
-
-
-def longitude_kernel(members, got_ref, base_ref, low_ref, out_ref):
+    re, im = 2.0 * jnp.cos(angle), 2.0 * jnp.sin(angle)
+    first = jnp.where(high == 0, 0.5, 1.0).astype(jnp.float32)
+    shape = (-(-FOLD // 8) * 8, LANES)
+    low = lax.broadcasted_iota(jnp.int32, shape, 0) * lax.broadcasted_iota(jnp.int32, shape, 1)
+    low = low.astype(jnp.float32) * (2.0 * math.pi / NLON)
+    cos, sin = jnp.cos(low), jnp.sin(low)
+    for q in range(FOLD):
+        cl, sl = cos[q : q + 1], sin[q : q + 1]
+        real, imag = re * cl - im * sl, im * cl + re * sl
+        if q == 0:
+            real, imag = real * first, imag * first
+        table_ref[q, :, :LANES] = real.astype(jnp.bfloat16)
+        table_ref[q, :, LANES:] = imag.astype(jnp.bfloat16)
+
+
+def longitude_kernel(members, got_ref, table_ref, out_ref):
     own = got_ref.shape[1]
     for i in range(own):
         spread = got_ref[:, i].astype(jnp.float32)
@@ -76,14 +88,9 @@
         turned = spread.T.astype(jnp.bfloat16)
         totals = [None] * FOLD
         for q in range(FOLD):
-            re, im = base_ref[0], base_ref[1]
-            if q == 0:
-                re, im = re * base_ref[2], im * base_ref[2]
-            cl, sl = low_ref[0, q : q + 1], low_ref[1, q : q + 1]
-            table = jnp.concatenate([re * cl - im * sl, im * cl + re * sl], axis=1)
             part = jnp.dot(
                 turned[q * members : (q + 1) * members],
-                table.astype(jnp.bfloat16),
+                table_ref[q],
                 preferred_element_type=jnp.float32,
             )
             real, imag = part[:, :LANES], part[:, LANES:]
@@ -96,9 +103,12 @@
 
 
 def coarse_kernel(
-    part_modes, decay_ref, amp_ref, state_ref, noise_ref, basis_ref, next_ref, mixed_ref
+    part_modes, decay_ref, amp_ref, state_ref, noise_ref, basis_ref, next_ref, mixed_ref, fine_ref, medium_ref
 ):
     held, parts, modes, slots = state_ref.shape
+    for scale, rate_ref in ((0, fine_ref), (1, medium_ref)):
+        rate_ref[0:1] = jnp.full((1, rate_ref.shape[1]), decay_ref[scale], jnp.float32)
+        rate_ref[1:2] = jnp.full((1, rate_ref.shape[1]), amp_ref[scale], jnp.float32)
     mode_ids = lax.broadcasted_iota(jnp.int32, (modes, slots), 0)
     degree_ids = lax.broadcasted_iota(jnp.int32, (modes, slots), 1)
     inside = mode_ids + degree_ids < slots
@@ -145,23 +155,25 @@
     part_modes = -(-modes // devices)
     vmem = pl.BlockSpec(memory_space=pltpu.VMEM)
     smem = pl.BlockSpec(memory_space=pltpu.SMEM)
-    coarse_next, mixed = pl.pallas_call(
+    coarse_next, mixed, fine_rates, medium_rates = pl.pallas_call(
         functools.partial(coarse_kernel, part_modes),
         out_shape=(
             jax.ShapeDtypeStruct(coarse_state.shape, jnp.float32),
             jax.ShapeDtypeStruct((devices, (2 * held + own) * part_modes, slots), jnp.bfloat16),
+            jax.ShapeDtypeStruct((2, fine_state.shape[3]), jnp.float32),
+            jax.ShapeDtypeStruct((2, medium_state.shape[3]), jnp.float32),
         ),
         in_specs=[smem, smem, vmem, vmem, vmem],
-        out_specs=(vmem, vmem),
+        out_specs=(vmem,) * 4,
     )(decay, amplitude, coarse_state, coarse_noise, coarse_basis)
     mixed = lax.all_to_all(mixed, ("scale", "lat"), split_axis=0, concat_axis=0, tiled=True)
     mixed = mixed.reshape(devices, 2 * held + own, part_modes, slots)
     coarse_half = mixed[:lat, : 2 * held].reshape(lat * held, 2, part_modes, slots)
     coarse_rows = mixed[:, 2 * held :].reshape(devices * own, part_modes, slots)
     place = lax.axis_index(("scale", "lat"))
-    fine_next = advance(fine_state, fine_noise, decay[0], amplitude[0], place * fine_state.shape[2])
+    fine_next = advance(fine_state, fine_noise, fine_rates[0], fine_rates[1], place * fine_state.shape[2])
     medium_next = advance(
-        medium_state, medium_noise, decay[1], amplitude[1], place * medium_state.shape[2]
+        medium_state, medium_noise, medium_rates[0], medium_rates[1], place * medium_state.shape[2]
     )
     fourier = []
     for half, basis, form in (
@@ -177,15 +189,26 @@
     both = jnp.concatenate([phase_blocks(x, place, devices) for x in fourier], axis=1)
     width = -(-both.shape[1] // 8) * 8
     both = jnp.pad(both, ((0, 0), (0, width - both.shape[1]), (0, 0)))
+    received = received_rows(blocks, devices, width)
+    table = pl.pallas_call(
+        table_kernel,
+        out_shape=jax.ShapeDtypeStruct((FOLD, devices * width, 2 * LANES), jnp.bfloat16),
+        in_specs=[vmem],
+        out_specs=vmem,
+        cost_estimate=pl.CostEstimate(
+            flops=30 * FOLD * devices * width * LANES,
+            bytes_accessed=8 * FOLD * devices * width * LANES,
+            transcendentals=4 * devices * width * LANES,
+        ),
+    )(jnp.asarray(received))
     got = lax.all_to_all(both, ("scale", "lat"), split_axis=0, concat_axis=0, tiled=True)
     got = got.reshape(devices, own, width, FOLD * members)
-    base, low = base_phases(blocks, devices, width)
     pattern = pl.pallas_call(
         functools.partial(longitude_kernel, members),
         out_shape=jax.ShapeDtypeStruct((members, own, NLON), jnp.float32),
-        in_specs=[vmem, vmem, vmem],
+        in_specs=[vmem, vmem],
         out_specs=vmem,
-    )(got, base, low)
+    )(got, table)
     return (fine_next, medium_next, coarse_next, pattern)
 
 

time: 62.7 us -> 54.9 us (0.88)
  other arithmetic: 23.2 us -> 13.3 us
  Pallas kernels: 4.77 us -> 9.46 us
  local copies, waits for them, and re-layouts: 11.9 us -> 8.99 us
  matrix products: 1.84 us -> 3.94 us
  waiting for transfers between devices: 6.43 us -> 4.78 us
    pallas_call x0 -> x1, Pallas kernels: none -> 4.17 us  [body(): pl.pallas_call(table_kernel, out_shape=jax.ShapeDtypeStruct((FOLD, device...]
    another operation x2 -> x0, other arithmetic: 3.07 us -> none  [the longest x1 1.74 us: base_phases(): jnp.stack([2.0 * jnp.cos(angle), 2.0 * jnp.sin(angle), first])]
    convert_element_type x1, other arithmetic: 5.52 us -> 2.8 us  [body(): medium_next.astype(jnp.bfloat16)]
    dot_general x3, matrix products: 1.84 us -> 3.94 us  [body(): jnp.einsum(form, half, basis, preferred_element_type=jnp.float32)]
    mul x1 -> x0, other arithmetic: 2.01 us -> none  [base_phases(): 2.0 * jnp.cos(angle)]
    all_to_all x1, waiting for transfers between devices: 6.42 us -> 4.78 us  [body(): lax.all_to_all(both, ('scale', 'lat'), split_axis=0, concat_axis=0, tiled...]
    concatenate x2 -> x0, local copies, waits for them, and re-layouts: 1.37 us -> none  [base_phases(): high = jnp.concatenate(cols, axis=1).reshape(-1, 1)]
    convert_element_type x1, other arithmetic: 9.22 us -> 7.86 us  [body(): fine_next.astype(jnp.bfloat16)]
  transfers between devices with their start and end apart: 2 -> 2, of which waited for: 1 -> 1; matrix products, arithmetic and copies ran while one was open for 55% -> 43% of each run, Pallas kernels for 0% -> 8%
where the time goes in v3:
time: 54.9 us; the launch traced here: 54.3 us
  other arithmetic  13.3 us (24%)
  starting transfers between devices  13.2 us (24%)
  Pallas kernels  9.46 us (17%)
  local copies, waits for them, and re-layouts  8.99 us (16%)
  waiting for transfers between devices  4.78 us (9%)
  matrix products  3.94 us (7%)
  between operations  0.74 us (1%)
    convert_element_type x1, other arithmetic, body(): fine_next.astype(jnp.bfloat16)  7.86 us
    all_to_all x1, starting transfers between devices, body(): lax.all_to_all(mixed, ('scale', 'lat'), split_axis=0, concat_axis=0, tile...  7.33 us
    all_to_all x1, starting transfers between devices, body(): lax.all_to_all(both, ('scale', 'lat'), split_axis=0, concat_axis=0, tiled...  5.83 us
    all_to_all x1, waiting for transfers between devices, body(): lax.all_to_all(both, ('scale', 'lat'), split_axis=0, concat_axis=0, tiled...  4.78 us
    pallas_call x1, Pallas kernels, body(): pl.pallas_call(table_kernel, out_shape=jax.ShapeDtypeStruct((FOLD, device...  4.17 us
    dot_general x3, matrix products, body(): jnp.einsum(form, half, basis, preferred_element_type=jnp.float32)  3.94 us
    reshape x3, local copies, waits for them, and re-layouts, phase_blocks(): return fourier.reshape(rows, parts * high, FOLD * members)  3.55 us
    pallas_call x1, Pallas kernels, body(): pl.pallas_call(functools.partial(longitude_kernel, members), out_shape=ja...  3.14 us
  transfers between devices with their start and end apart: 2, of which 1 were waited for; matrix products, arithmetic and copies ran while one was open for 43% of the time, Pallas kernels for 8%

profile of v3, /device:TPU:0, one launch (start us, length us, event | category | flops | bytes accessed | tf_op | source)
XLA Modules:
  0.0 54.3 jit_solution(7914022533490892389)
XLA Ops:
  0.6 0.0 copy-start
  0.6 2.2 %shard_map.147 = (f32[1,2,160,160]{3,2,1,0:T(8,128)}, bf16[32,15,160]{2,1,0:T(8,128)(2,1)}, f32[2,1280]{1,0:T(2,128)}, f32[2,640]{1,0:T(2,128)}) custom-call(f32[3]{0:T(128)} %decay_ref.1, f32[3]{0:T(128)} %amp_ref.1, f32[1,2,160,160]{3,2,1,0:T(8,128)} %state_ref.1, bf16[1,2,160,160]{3,2,1,0:T(8,128)(2,1)} %noise_ref.1, bf16[1,160,160]{2,1,0:T(8,128)(2,1)} %basis_ref.1), custom_call_target="tpu_custom_call" | custom-call | tf_op jit(solution)/shard_map/pallas_call | solution.py:158
  2.8 7.3 %all-to-all-start = ((bf16[32,15,160]{2,1,0:T(8,128)(2,1)}), bf16[32,15,160]{2,1,0:T(8,128)(2,1)S(1)}, u32[]{:S(2)}, u32[]{:S(2)}) async-start(bf16[32,15,160]{2,1,0:T(8,128)(2,1)} %get-tuple-element.11), calls=%async_computation | async-start | bytes 524288 | tf_op jit(solution)/shard_map/all_to_all | solution.py:169
  10.1 0.8 %slice_reduce_fusion.1 = (f32[1280]{0:T(1024)S(1)}, f32[1280]{0:T(1024)S(1)}) fusion(f32[2,1280]{1,0:T(2,128)} %get-tuple-element.8), kind=kLoop, calls=%fused_computation.20 | loop fusion | bytes 20480 | tf_op jit(solution)/shard_map/slice | solution.py:174
  11.0 0.7 %add_compare_fusion = pred[40,1280]{1,0:T(8,128)(4,1)} fusion(s32[40]{0:T(128)S(1)} %iota_add_fusion.1), kind=kLoop, calls=%fused_computation.13 | loop fusion | flops 102400 | bytes 51360 | tf_op jit(solution)/shard_map/lt | solution.py:21
  11.7 1.4 %slice_reduce_fusion.3 = (f32[640]{0:T(1024)}, f32[640]{0:T(1024)}) fusion(f32[2,640]{1,0:T(2,128)} %get-tuple-element.9), kind=kLoop, calls=%fused_computation.22 | loop fusion | bytes 10240 | tf_op jit(solution)/shard_map/slice | solution.py:176
  13.1 0.1 add_compare_fusion.1
  13.2 7.9 %fusion.18 = (bf16[16,2,40,1280]{3,2,1,0:T(8,128)(2,1)S(1)}, f32[16,2,40,1280]{3,2,1,0:T(8,128)}) fusion(bf16[16,2,40,1280]{3,2,1,0:T(8,128)(2,1)} %param.13, f32[1280]{0:T(1024)S(1)} %get-tuple-element.13, f32[16,2,40,1280]{3,2,1,0:T(8,128)} %param.12, f32[1280]{0:T(1024)S(1)} %get-tuple-element.12, pred[40,1280]{1,0:T(8,128)(4,1)} %add_compare_fusion), kind=kLoop, calls=%fused_computation.25 | loop fusion | flops 9830400 | bytes 19722240 | tf_op jit(solution)/shard_map/convert_element_type | solution.py:180
  21.0 0.0 copy-done
  21.0 0.0 copy-start.1
  21.0 0.0 copy-start.5
  21.0 2.0 %fusion.8 = bf16[32,2,40,16]{0,3,1,2:T(8,128)(2,1)} fusion(bf16[40,32,1280]{2,1,0:T(8,128)(2,1)S(1)} %copy-done, bf16[16,2,40,1280]{3,2,1,0:T(8,128)(2,1)S(1)} %get-tuple-element.16), kind=kOutput, calls=%fused_computation.6 | convolution fusion | flops 104898560 | bytes 6635520 | tf_op jit(solution)/shard_map/ecmk,mrk->rcme/dot_general | solution.py:185
  23.1 0.0 copy-done.1
  23.1 0.0 copy-done.2
  23.1 0.0 copy-done.4
  23.1 0.0 copy-done.5
  23.1 2.8 %fusion.19 = (bf16[16,2,20,640]{3,1,2,0:T(2,128)(2,1)}, f32[16,2,20,640]{3,1,2,0:T(2,128)}) fusion(bf16[16,2,20,640]{3,1,2,0:T(2,128)(2,1)S(1)} %copy-done.2, f32[640]{0:T(1024)S(1)} %copy-done.5, f32[16,2,20,640]{3,1,2,0:T(2,128)S(1)} %copy-done.1, f32[640]{0:T(1024)S(1)} %copy-done.4, pred[20,640]{1,0:T(8,128)(4,1)S(1)} %add_compare_fusion.1), kind=kLoop, calls=%fused_computation.26 | loop fusion | flops 2457600 | bytes 4933120 | tf_op jit(solution)/shard_map/convert_element_type | solution.py:181
  25.9 1.7 %copy.24 = bf16[32,2,40,16]{0,3,2,1:T(8,128)(2,1)} copy(bf16[32,2,40,16]{0,3,1,2:T(8,128)(2,1)} %fusion.8) | data formatting | bytes 163840 | tf_op jit(solution)/shard_map/convert_element_type | solution.py:185
  27.6 1.8 %copy.30 = bf16[32,4,320]{2,1,0:T(4,128)(2,1)} copy(bf16[32,4,320]{0,2,1:T(8,128)(2,1)} %bitcast.31) | data formatting | bytes 163840 | tf_op jit(solution)/shard_map/reshape | solution.py:38
  29.4 1.8 %fusion.13 = bf16[32,2,20,16]{0,3,1,2:T(8,128)(2,1)S(1)} fusion(bf16[20,32,640]{2,1,0:T(8,128)(2,1)} %param.21, bf16[16,2,20,640]{3,1,2,0:T(2,128)(2,1)} %get-tuple-element.18), kind=kOutput, calls=%fused_computation.8 | convolution fusion | flops 26234880 | bytes 1679360 | tf_op jit(solution)/shard_map/ecmk,mrk->rcme/dot_general | solution.py:185
  31.2 0.7 %copy.26 = bf16[32,2,20,16]{0,3,2,1:T(8,128)(2,1)} copy(bf16[32,2,20,16]{0,3,1,2:T(8,128)(2,1)S(1)} %fusion.13) | data formatting | bytes 81920 | tf_op jit(solution)/shard_map/convert_element_type | solution.py:185
  31.9 1.7 %copy.31 = bf16[32,2,320]{2,1,0:T(2,128)(2,1)} copy(bf16[32,2,320]{0,2,1:T(8,128)(2,1)} %bitcast.34) | data formatting | bytes 81920 | tf_op jit(solution)/shard_map/reshape | solution.py:38
  33.5 0.0 all-to-all-done
  33.5 0.1 copy.27
  33.6 0.1 fusion.14
  33.8 0.1 copy.32
  33.9 1.8 %pad_maximum_fusion = bf16[32,8,320]{2,1,0:T(8,128)(2,1)} fusion(bf16[32,2,320]{2,1,0:T(2,128)(2,1)S(1)} %copy.32, bf16[32,2,320]{2,1,0:T(2,128)(2,1)} %copy.31, bf16[32,4,320]{2,1,0:T(4,128)(2,1)} %copy.30), kind=kLoop, calls=%fused_computation.14 | loop fusion | flops 491520 | bytes 327680 | tf_op jit(solution)/shard_map/concatenate | solution.py:189
  35.7 5.8 %all-to-all-start.1 = ((bf16[32,8,320]{2,1,0:T(8,128)(2,1)}), bf16[32,8,320]{2,1,0:T(8,128)(2,1)S(1)}, u32[]{:S(2)}, u32[]{:S(2)}) async-start(bf16[32,8,320]{2,1,0:T(8,128)(2,1)} %pad_maximum_fusion), calls=%async_computation.1 | async-start | bytes 393216 | tf_op jit(solution)/shard_map/all_to_all | solution.py:204
  41.6 4.2 %shard_map.148.table_ref = bf16[20,256,256]{2,1,0:T(8,128)(2,1)} custom-call(s32[256,2]{1,0:T(8,128)} %constant.37.clone.rows_ref), custom_call_target="tpu_custom_call" | custom-call | flops 19660800 | bytes 5242880 | tf_op jit(solution)/shard_map/pallas_call | solution.py:193
  45.7 4.8 %all-to-all-done.1 = bf16[32,8,320]{2,1,0:T(8,128)(2,1)S(1)} async-done(((bf16[32,8,320]{2,1,0:T(8,128)(2,1)}), bf16[32,8,320]{2,1,0:T(8,128)(2,1)S(1)}, u32[]{:S(2)}, u32[]{:S(2)}) %all-to-all-start.1) | async-done | bytes 163872 | tf_op jit(solution)/shard_map/all_to_all | solution.py:204
  50.5 0.7 %copy-done.3 = bf16[32,8,320]{2,1,0:T(8,128)(2,1)} copy-done((bf16[32,8,320]{2,1,0:T(8,128)(2,1)}, bf16[32,8,320]{2,1,0:T(8,128)(2,1)S(1)}, u32[]{:S(2)}) %copy-start.3) | copy-done | bytes 163864
  51.2 3.1 %shard_map.149 = f32[16,1,2560]{2,1,0:T(1,128)} custom-call(bf16[32,1,8,320]{3,2,1,0:T(8,128)(2,1)} %bitcast.32, bf16[20,256,256]{2,1,0:T(8,128)(2,1)} %shard_map.148.table_ref), custom_call_target="tpu_custom_call" | custom-call | tf_op jit(solution)/shard_map/pallas_call | solution.py:206
  (7 shorter events, 0.1 us)
Async XLA Ops:
  0.6 20.4 %copy-start = (bf16[40,32,1280]{2,1,0:T(8,128)(2,1)S(1)}, bf16[40,32,1280]{2,1,0:T(8,128)(2,1)}, u32[]{:S(2)}) copy-start(bf16[40,32,1280]{2,1,0:T(8,128)(2,1)} %param.20) | copy-start | bytes 9830404
  2.8 30.7 %all-to-all-start = ((bf16[32,15,160]{2,1,0:T(8,128)(2,1)}), bf16[32,15,160]{2,1,0:T(8,128)(2,1)S(1)}, u32[]{:S(2)}, u32[]{:S(2)}) async-start(bf16[32,15,160]{2,1,0:T(8,128)(2,1)} %get-tuple-element.11), calls=%async_computation | async-start | bytes 524288 | tf_op jit(solution)/shard_map/all_to_all | solution.py:169
  21.0 2.1 %copy-start.1 = (f32[16,2,20,640]{3,1,2,0:T(2,128)S(1)}, f32[16,2,20,640]{3,1,2,0:T(2,128)}, u32[]{:S(2)}) copy-start(f32[16,2,20,640]{3,1,2,0:T(2,128)} %param.14) | copy-start | bytes 4915204
  21.0 2.1 %copy-start.2 = (bf16[16,2,20,640]{3,1,2,0:T(2,128)(2,1)S(1)}, bf16[16,2,20,640]{3,1,2,0:T(2,128)(2,1)}, u32[]{:S(2)}) copy-start(bf16[16,2,20,640]{3,1,2,0:T(2,128)(2,1)} %param.15) | copy-start | bytes 2457604
  21.0 2.1 %copy-start.4 = (f32[640]{0:T(1024)S(1)}, f32[640]{0:T(1024)}, u32[]{:S(2)}) copy-start(f32[640]{0:T(1024)} %get-tuple-element.14) | copy-start | bytes 7684
  21.0 2.1 %copy-start.5 = (f32[640]{0:T(1024)S(1)}, f32[640]{0:T(1024)}, u32[]{:S(2)}) copy-start(f32[640]{0:T(1024)} %get-tuple-element.15) | copy-start | bytes 7684
  35.7 14.8 %all-to-all-start.1 = ((bf16[32,8,320]{2,1,0:T(8,128)(2,1)}), bf16[32,8,320]{2,1,0:T(8,128)(2,1)S(1)}, u32[]{:S(2)}, u32[]{:S(2)}) async-start(bf16[32,8,320]{2,1,0:T(8,128)(2,1)} %pad_maximum_fusion), calls=%async_computation.1 | async-start | bytes 393216 | tf_op jit(solution)/shard_map/all_to_all | solution.py:204
  50.5 0.7 %copy-start.3 = (bf16[32,8,320]{2,1,0:T(8,128)(2,1)}, bf16[32,8,320]{2,1,0:T(8,128)(2,1)S(1)}, u32[]{:S(2)}) copy-start(bf16[32,8,320]{2,1,0:T(8,128)(2,1)S(1)} %all-to-all-done.1) | copy-start | bytes 491524
